TPU v7x, 256 devices: a whole 4x4x8 slice. The times are simulated.
256 devices in a mesh: grid: 64 (over z, x, core), band: 4 (over y).
Axes of the slice: x: 4, y: 4, z: 8, core: 2. Of those that a mesh axis runs over, the one named last changes fastest.
Arguments:
- basis: float32 [2048, 65536], P('band', 'grid'), as said below
- panel: float32 [1024, 65536], P('band', 'grid'), may hold values from -6 to 6
Outputs:
- new_panel: float32 [1024, 65536], P('band', 'grid')
- coeffs: float32 [2048, 1024], P('band')
Inputs may be any that keep to these rules, and one draw needn't show every extreme that they name: The rows of basis are orthogonal to each other, each with squared sum 65536 (to float32 rounding).
All inputs are finite; a program needn't handle non-finite values.
Results may differ from a plain program's by a relative error of at most 0.000073.
Values sent between devices are 32-bit elements; how exact they have to be, the bound alone decides.
A program may use at most 128 MiB of HBM per device.

v0:
```python
import jax
import jax.numpy as jnp
from jax import lax
from jax.sharding import PartitionSpec as P


def together(arrays, axis):
    ravelled, at, finished = (jnp.concatenate([a.reshape(-1) for a in arrays]), 0, [])
    total = lax.psum(ravelled, axis)
    for a in arrays:
        finished.append(total[at : at + a.size].reshape(a.shape))
        at += a.size
    return tuple(finished)


def cut_along(array, dim, count):
    before, after = (array.shape[:dim], array.shape[dim + 1 :])
    return jnp.moveaxis(array.reshape(*before, count, -1, *after), dim, 0)


def summed_on_arrival(array, axis, dim):
    blocks = cut_along(array, dim, lax.axis_size(axis))
    arrived = lax.all_to_all(blocks, axis, split_axis=0, concat_axis=0, tiled=True)
    return arrived.sum(axis=0)


def tdot(left, right):
    return lax.dot_general(
        left,
        right,
        (((1,), (1,)), ((), ())),
        precision=lax.Precision.HIGHEST,
        preferred_element_type=jnp.float32,
    )


def ndot(left, right):
    return jnp.dot(left, right, precision=lax.Precision.HIGHEST)


def body(basis, panel):
    n_grid = panel.shape[1] * lax.axis_size("grid")
    n_band = lax.axis_size("band")
    rows_q = basis.shape[0]
    rows_p = panel.shape[0]
    n_panel = rows_p * n_band
    stacked = jnp.concatenate([basis, panel], 0)
    both = tdot(stacked, lax.all_gather(panel, "band", axis=0, tiled=True))
    coeff_sum, gram_sum = together((both[:rows_q], both[rows_q:]), "grid")
    coeffs = coeff_sum / n_grid
    projected = panel - lax.psum_scatter(
        ndot(coeffs.T, basis), "band", scatter_dimension=0, tiled=True
    )
    gram_part = gram_sum / n_grid - summed_on_arrival(ndot(coeffs.T, coeffs), "band", 0)
    gram = lax.all_gather(gram_part, "band", axis=0, tiled=True)
    factor = jnp.linalg.cholesky(gram)
    offset = lax.axis_index("band") * rows_p
    row_ids = lax.broadcasted_iota(jnp.int32, (n_panel, rows_p), 0)
    col_ids = lax.broadcasted_iota(jnp.int32, (n_panel, rows_p), 1)
    unit_cols = (row_ids == col_ids + offset).astype(jnp.float32)
    inverse_rows = lax.linalg.triangular_solve(
        factor, unit_cols, left_side=True, lower=True, transpose_a=True
    ).T
    new_panel = ndot(inverse_rows, lax.all_gather(projected, "band", axis=0, tiled=True))
    return (new_panel, coeffs)


def solution(mesh):
    placed = (P("band", "grid"), P("band", "grid"))
    return jax.shard_map(
        body,
        mesh=mesh,
        in_specs=placed,
        out_specs=(P("band", "grid"), P("band", None)),
        check_vma=False,
    )
```

profile of v0, /device:TPU:1, one launch (start us, length us, event | category | flops | bytes accessed | tf_op | source)
XLA Modules:
  0.0 783.9 jit_solution(712397003574629770)
XLA Ops:
  7.9 56.3 %all-gather.4.cloned.1.call-done = f32[1024,1024]{1,0:T(8,128)} async-done(((f32[256,1024]{1,0:T(8,128)}), f32[1024,1024]{1,0:T(8,128)}) %all-gather.4.cloned.1.call-update) | async-done | bytes 4194320 | tf_op jit(solution)/shard_map/all_gather | solution.py:48
  64.2 12.5 %fusion.1 = f32[768,1024]{1,0:T(8,128)S(1)} fusion(f32[1024,1024]{1,0:T(8,128)} %all-gather.4.cloned.1.call-done, f32[256,1024]{1,0:T(8,128)} %param.3, f32[512,1024]{1,0:T(8,128)} %param.2), kind=kOutput, calls=%fused_computation.6 | convolution fusion | flops 9664462848 | bytes 10485760 | tf_op jit(solution)/shard_map/dot_general | solution.py:28
  79.8 191.7 %all-reduce.3.cloned.1.call-done = f32[786432]{0:T(1024)} async-done(((f32[786432]{0:T(1024)}), f32[786432]{0:T(1024)}) %all-reduce.3.cloned.1.call-update) | async-done | bytes 3145744 | tf_op jit(solution)/shard_map/psum | solution.py:9
  274.7 10.2 %fusion.69 = f32[1024,1024]{1,0:T(8,128)} fusion(f32[512,1024]{1,0:T(8,128)} %div.29, f32[512,1024]{1,0:T(8,128)} %param.2), kind=kOutput, calls=%fused_computation.169 | convolution fusion | flops 6442450944 | bytes 8388608 | tf_op jit(solution)/shard_map/dot_general | solution.py:38
  286.4 3.1 copy.13
  289.5 9.9 %fusion.68 = f32[4,256,1024]{2,1,0:T(8,128)} fusion(f32[4,256,512]{2,1,0:T(8,128)} %bitcast.110, f32[512,1024,1]{1,0,2:T(8,128)S(1)} %copy-done.2), kind=kOutput, calls=%fused_computation.168 | convolution fusion | flops 6442450944 | bytes 8388608 | tf_op jit(solution)/shard_map/dot_general | solution.py:38
  299.4 4.9 all-to-all-start
  306.2 72.1 %all-to-all-done = f32[4,256,1024]{2,1,0:T(8,128)} async-done(((f32[4,256,1024]{2,1,0:T(8,128)}), f32[4,256,1024]{2,1,0:T(8,128)}, u32[]{:S(2)}, u32[]{:S(2)}) %all-to-all-start) | async-done | bytes 4194336 | tf_op jit(solution)/shard_map/all_to_all | solution.py:23
  378.3 3.7 reduce_sum.9
  385.1 2.4 sub.7
  387.5 48.0 %all-gather.6.cloned.1.call-done = f32[1024,1024]{0,1:T(8,128)} async-done(((f32[256,1024]{0,1:T(8,128)}), f32[1024,1024]{0,1:T(8,128)}) %all-gather.6.cloned.1.call-update) | async-done | bytes 4194320 | tf_op jit(solution)/shard_map/all_gather | solution.py:55
  435.5 5.5 copy.12
  441.1 4.4 fusion
  447.5 11.7 %cholesky.223 = f32[128,128]{1,0:T(8,128)S(1)} custom-call(f32[128,128]{1,0:T(8,128)S(1)} %cholesky.580), custom_call_target="Cholesky" | custom-call | tf_op jit(solution)/shard_map/jit(cholesky)/cholesky | solution.py:56
  459.2 2.5 cholesky.255
  461.8 9.8 %custom-call.62 = f32[1,128,128]{1,2,0:T(8,128)S(1)} custom-call(f32[1,128,128]{2,1,0:T(8,128)S(1)} %get-tuple-element.41), custom_call_target="InvertDiagBlocksLowerTriangular" | custom-call | tf_op jit(solution)/shard_map/jit(cholesky)/cholesky | solution.py:56
  471.6 2.4 constant_dynamic-update-slice_fusion.32
  475.5 12.1 %cholesky.244 = f32[128,128]{1,0:T(8,128)S(1)} custom-call(f32[128,128]{1,0:T(8,128)S(1)} %cholesky.584), custom_call_target="Cholesky" | custom-call | tf_op jit(solution)/shard_map/jit(cholesky)/cholesky | solution.py:56
  488.2 9.8 %custom-call.63 = f32[1,128,128]{1,2,0:T(8,128)S(1)} custom-call(f32[1,128,128]{2,1,0:T(8,128)S(1)} %get-tuple-element.38), custom_call_target="InvertDiagBlocksLowerTriangular" | custom-call | tf_op jit(solution)/shard_map/jit(cholesky)/cholesky | solution.py:56
  499.3 2.1 convolution_subtract_fusion.1
  501.4 11.7 %cholesky.468 = f32[128,128]{1,0:T(8,128)S(1)} custom-call(f32[128,128]{1,0:T(8,128)S(1)} %cholesky.589), custom_call_target="Cholesky" | custom-call | tf_op jit(solution)/shard_map/jit(cholesky)/cholesky | solution.py:56
  514.4 9.8 %custom-call.64 = f32[1,128,128]{1,2,0:T(8,128)S(1)} custom-call(f32[1,128,128]{2,1,0:T(8,128)S(1)} %get-tuple-element.35), custom_call_target="InvertDiagBlocksLowerTriangular" | custom-call | tf_op jit(solution)/shard_map/jit(cholesky)/cholesky | solution.py:56
  525.4 2.3 convolution_subtract_fusion.2
  527.7 11.8 %cholesky.487 = f32[128,128]{1,0:T(8,128)S(1)} custom-call(f32[128,128]{1,0:T(8,128)S(1)} %cholesky.594), custom_call_target="Cholesky" | custom-call | tf_op jit(solution)/shard_map/jit(cholesky)/cholesky | solution.py:56
  540.8 9.8 %custom-call.65 = f32[1,128,128]{1,2,0:T(8,128)S(1)} custom-call(f32[1,128,128]{2,1,0:T(8,128)S(1)} %get-tuple-element.32), custom_call_target="InvertDiagBlocksLowerTriangular" | custom-call | tf_op jit(solution)/shard_map/jit(cholesky)/cholesky | solution.py:56
  551.8 2.4 convolution_subtract_fusion.3
  554.1 11.7 %cholesky.506 = f32[128,128]{1,0:T(8,128)S(1)} custom-call(f32[128,128]{1,0:T(8,128)S(1)} %cholesky.599), custom_call_target="Cholesky" | custom-call | tf_op jit(solution)/shard_map/jit(cholesky)/cholesky | solution.py:56
  567.2 10.0 %custom-call.66 = f32[1,128,128]{1,2,0:T(8,128)S(1)} custom-call(f32[1,128,128]{2,1,0:T(8,128)S(1)} %get-tuple-element.29), custom_call_target="InvertDiagBlocksLowerTriangular" | custom-call | tf_op jit(solution)/shard_map/jit(cholesky)/cholesky | solution.py:56
  578.2 2.3 convolution_subtract_fusion.4
  580.5 11.7 %cholesky.526 = f32[128,128]{1,0:T(8,128)S(1)} custom-call(f32[128,128]{1,0:T(8,128)S(1)} %cholesky.604), custom_call_target="Cholesky" | custom-call | tf_op jit(solution)/shard_map/jit(cholesky)/cholesky | solution.py:56
  593.4 9.8 %custom-call.67 = f32[1,128,128]{1,2,0:T(8,128)S(1)} custom-call(f32[1,128,128]{2,1,0:T(8,128)S(1)} %get-tuple-element.26), custom_call_target="InvertDiagBlocksLowerTriangular" | custom-call | tf_op jit(solution)/shard_map/jit(cholesky)/cholesky | solution.py:56
  604.2 2.0 convolution_subtract_fusion.11
  606.2 12.1 %cholesky.546 = f32[128,128]{1,0:T(8,128)S(1)} custom-call(f32[128,128]{1,0:T(8,128)S(1)} %cholesky.609), custom_call_target="Cholesky" | custom-call | tf_op jit(solution)/shard_map/jit(cholesky)/cholesky | solution.py:56
  619.7 9.8 %custom-call.68 = f32[1,128,128]{1,2,0:T(8,128)S(1)} custom-call(f32[1,128,128]{2,1,0:T(8,128)S(1)} %get-tuple-element.23), custom_call_target="InvertDiagBlocksLowerTriangular" | custom-call | tf_op jit(solution)/shard_map/jit(cholesky)/cholesky | solution.py:56
  632.1 11.7 %cholesky.564 = f32[128,128]{1,0:T(8,128)S(1)} custom-call(f32[128,128]{1,0:T(8,128)S(1)} %convolution_subtract_fusion.13), custom_call_target="Cholesky" | custom-call | tf_op jit(solution)/shard_map/jit(cholesky)/cholesky | solution.py:56
  650.7 4.8 select_select_fusion
  655.5 22.6 %while.1 = (s32[]{:T(128)}, f32[1024,1024]{1,0:T(8,128)}, s32[8,2]{0,1:T(2,128)S(1)}, f32[8,128,128]{2,1,0:T(8,128)S(1)}, s32[]{:T(128)}) while((s32[]{:T(128)}, f32[1024,1024]{1,0:T(8,128)}, s32[8,2]{0,1:T(2,128)S(1)}, f32[8,128,128]{2,1,0:T(8,128)S(1)}, s32[]{:T(128)}) %tuple.43), condition=%wide.while_cond, body=%wide.while_body.sunk | while | flops 2 | bytes 131181 | solution.py:61
  656.1 2.2 bitcast_dynamic-update-slice_fusion.2
  658.9 2.2 bitcast_dynamic-update-slice_fusion.2
  661.8 2.2 bitcast_dynamic-update-slice_fusion.2
  664.6 2.2 bitcast_dynamic-update-slice_fusion.2
  667.4 2.2 bitcast_dynamic-update-slice_fusion.2
  670.3 2.2 bitcast_dynamic-update-slice_fusion.2
  673.1 2.2 bitcast_dynamic-update-slice_fusion.2
  675.9 2.1 bitcast_dynamic-update-slice_fusion.2
  678.1 78.8 %custom-call.69 = f32[8,128,128]{1,2,0:T(8,128)S(1)} custom-call(f32[8,128,128]{2,1,0:T(8,128)S(1)} %get-tuple-element.9), custom_call_target="InvertDiagBlocksLowerTriangular" | custom-call | tf_op jit(solution)/shard_map/triangular_solve | solution.py:61
  768.0 2.0 convolution_subtract_fusion.12
  770.4 6.8 fusion.70
  (118 shorter events, 50.1 us)
Async XLA Ops:
  7.2 57.1 %all-gather.4.cloned.1.call-start = ((), (), s32[]{:S(2)}) async-start(), calls=%async_computation.2 | async-start | bytes 5242880 | tf_op jit(solution)/shard_map/all_gather | solution.py:48
  7.9 263.6 %all-reduce.3.cloned.1.call-start = ((), (), s32[]{:S(2)}) async-start(), calls=%async_computation.3 | async-start | bytes 6291456 | tf_op jit(solution)/shard_map/psum | solution.py:9
  79.5 305.5 %reduce-scatter.2.cloned.1.call-start = ((), (), s32[]{:S(2)}) async-start(), calls=%async_computation.5 | async-start | bytes 5242880 | tf_op jit(solution)/shard_map/reduce_scatter | solution.py:51
  286.4 3.1 copy-start.2
  299.4 78.9 %all-to-all-start = ((f32[4,256,1024]{2,1,0:T(8,128)}), f32[4,256,1024]{2,1,0:T(8,128)}, u32[]{:S(2)}, u32[]{:S(2)}) async-start(f32[4,256,1024]{2,1,0:T(8,128)} %fusion.68), calls=%async_computation | async-start | bytes 8388608 | tf_op jit(solution)/shard_map/all_to_all | solution.py:23
  304.4 131.2 %all-gather.6.cloned.1.call-start = ((), (), s32[]{:S(2)}) async-start(), calls=%async_computation.4 | async-start | bytes 5242880 | tf_op jit(solution)/shard_map/all_gather | solution.py:55
  382.0 3.1 copy-start.1
  384.7 385.7 %all-gather.8.cloned.1.call-start = ((), (), s32[]{:S(2)}) async-start(), calls=%async_computation.6 | async-start | bytes 5242880 | tf_op jit(solution)/shard_map/all_gather | solution.py:64
  445.5 2.0 copy-start
Sparse Core Ops, SparseCore 0:
  9.8 54.3 all-gather.3
  79.7 191.8 all-reduce.2
  285.1 73.5 reduce-scatter.1
  384.9 50.6 all-gather.5
  437.2 51.1 all-gather.7
where the time goes:
time: 790 us; the launch traced here: 784 us
  waiting for transfers between devices  369 us (47%)
  other arithmetic  273 us (35%)
  matrix products  75.5 us (10%)
  local copies, waits for them, and re-layouts  41.8 us (5%)
  between operations  19.4 us (2%)
    psum x1, waiting for transfers between devices, together(): total = lax.psum(ravelled, axis)  192 us
    another operation x30, other arithmetic, body(): factor = jnp.linalg.cholesky(gram)  172 us
    another operation x3, other arithmetic, body(): lax.linalg.triangular_solve(factor, unit_cols, left_side=True, lower=True...  83.6 us
    all_to_all x1, waiting for transfers between devices, summed_on_arrival(): lax.all_to_all(blocks, axis, split_axis=0, concat_axis=0, tiled=True)  72.1 us
    all_gather x1, waiting for transfers between devices, body(): both = tdot(stacked, lax.all_gather(panel, 'band', axis=0, tiled=True))  56.3 us
    all_gather x1, waiting for transfers between devices, body(): gram = lax.all_gather(gram_part, 'band', axis=0, tiled=True)  48 us
    dot_general x3, matrix products, ndot(): return jnp.dot(left, right, precision=lax.Precision.HIGHEST)  26.8 us
    another operation x14, matrix products, body(): factor = jnp.linalg.cholesky(gram)  23.1 us
  transfers between devices with their start and end apart: 6, of which 4 were waited for; matrix products, arithmetic and copies ran while one was open for 45% of the time, Pallas kernels for 0%

commit v1 on v0

--- a/solution.py
+++ b/solution.py
@@ -52,7 +52,25 @@
         ndot(coeffs.T, basis), "band", scatter_dimension=0, tiled=True
     )
     gram_part = gram_sum / n_grid - summed_on_arrival(ndot(coeffs.T, coeffs), "band", 0)
-    gram = lax.all_gather(gram_part, "band", axis=0, tiled=True)
+    count_2, index, width = (lax.axis_size("band"), lax.axis_index("band"), gram_part.shape[0])
+    route = [(i, (i + 1) % count_2) for i in range(count_2)]
+    backward = [(i, (i - 1) % count_2) for i in range(count_2)]
+    gram = jnp.zeros(
+        (*gram_part.shape[:0], count_2 * width, *gram_part.shape[0 + 1 :]), gram_part.dtype
+    )
+    gram = lax.dynamic_update_slice_in_dim(gram, gram_part, index * width, axis=0)
+    from_left = from_right = gram_part
+    middle = count_2 // 2
+    for step in range(1, middle + 1):
+        from_left = lax.ppermute(from_left, "band", route)
+        gram = lax.dynamic_update_slice_in_dim(
+            gram, from_left, (index - step) % count_2 * width, axis=0
+        )
+        if step < count_2 - middle:
+            from_right = lax.ppermute(from_right, "band", backward)
+            gram = lax.dynamic_update_slice_in_dim(
+                gram, from_right, (index + step) % count_2 * width, axis=0
+            )
     factor = jnp.linalg.cholesky(gram)
     offset = lax.axis_index("band") * rows_p
     row_ids = lax.broadcasted_iota(jnp.int32, (n_panel, rows_p), 0)

time: 790 us -> 802 us (1.015)
  the two profiles are of different devices: /device:TPU:1 before, /device:TPU:32 now
where the time goes in v1:
time: 802 us; the launch traced here: 793 us
  waiting for transfers between devices  359 us (45%)
  other arithmetic  267 us (33%)
  matrix products  76.6 us (10%)
  local copies, waits for them, and re-layouts  61.3 us (8%)
  between operations  19.8 us (2%)
  starting transfers between devices  8.41 us (1%)
    psum x1, waiting for transfers between devices, together(): total = lax.psum(ravelled, axis)  191 us
    another operation x30, other arithmetic, body(): factor = jnp.linalg.cholesky(gram)  167 us
    another operation x3, other arithmetic, body(): lax.linalg.triangular_solve(factor, unit_cols, left_side=True, lower=True...  84.3 us
    ppermute x2, waiting for transfers between devices, body(): from_left = lax.ppermute(from_left, 'band', route)  63.4 us
    all_gather x1, waiting for transfers between devices, body(): both = tdot(stacked, lax.all_gather(panel, 'band', axis=0, tiled=True))  55.3 us
    all_to_all x1, waiting for transfers between devices, summed_on_arrival(): lax.all_to_all(blocks, axis, split_axis=0, concat_axis=0, tiled=True)  48.1 us
    another operation x40, local copies, waits for them, and re-layouts  28 us
    another operation x14, matrix products, body(): factor = jnp.linalg.cholesky(gram)  27.5 us
  transfers between devices with their start and end apart: 8, of which 6 were waited for; matrix products, arithmetic and copies ran while one was open for 45% of the time, Pallas kernels for 0%

profile of v1, /device:TPU:32, one launch (start us, length us, event | category | flops | bytes accessed | tf_op | source)
XLA Modules:
  0.0 793.1 jit_solution(15723654454524131206)
XLA Ops:
  7.9 55.3 %all-gather.3.cloned.1.call-done = f32[1024,1024]{1,0:T(8,128)} async-done(((f32[256,1024]{1,0:T(8,128)}), f32[1024,1024]{1,0:T(8,128)}) %all-gather.3.cloned.1.call-update) | async-done | bytes 4194320 | tf_op jit(solution)/shard_map/all_gather | solution.py:48
  63.2 12.5 %fusion.1 = f32[768,1024]{1,0:T(8,128)S(1)} fusion(f32[1024,1024]{1,0:T(8,128)} %all-gather.3.cloned.1.call-done, f32[256,1024]{1,0:T(8,128)} %param.3, f32[512,1024]{1,0:T(8,128)} %param.2), kind=kOutput, calls=%fused_computation.6 | convolution fusion | flops 9664462848 | bytes 10485760 | tf_op jit(solution)/shard_map/dot_general | solution.py:28
  78.5 191.1 %all-reduce.3.cloned.1.call-done = f32[786432]{0:T(1024)} async-done(((f32[786432]{0:T(1024)}), f32[786432]{0:T(1024)}) %all-reduce.3.cloned.1.call-update) | async-done | bytes 3145744 | tf_op jit(solution)/shard_map/psum | solution.py:9
  274.3 3.1 copy.67
  277.4 9.9 %fusion.85 = f32[4,256,1024]{2,1,0:T(8,128)} fusion(f32[4,256,512]{2,1,0:T(8,128)} %bitcast.108, f32[512,1024,1]{1,0,2:T(8,128)S(1)} %copy-done.4), kind=kOutput, calls=%fused_computation.179 | convolution fusion | flops 6442450944 | bytes 8388608 | tf_op jit(solution)/shard_map/dot_general | solution.py:38
  287.3 4.8 all-to-all-start
  294.2 48.1 %all-to-all-done = f32[4,256,1024]{2,1,0:T(8,128)} async-done(((f32[4,256,1024]{2,1,0:T(8,128)}), f32[4,256,1024]{2,1,0:T(8,128)}, u32[]{:S(2)}, u32[]{:S(2)}) %all-to-all-start) | async-done | bytes 4194336 | tf_op jit(solution)/shard_map/all_to_all | solution.py:23
  342.3 2.7 reduce_sum.9
  345.4 2.7 broadcast_in_dim.5
  349.8 2.7 collective-permute-start.1
  352.4 8.4 %fusion.86 = f32[1024,1024]{1,0:T(8,128)} fusion(f32[512,1024]{1,0:T(8,128)S(1)} %copy-done, f32[512,1024]{1,0:T(8,128)S(1)} %copy-done.3), kind=kOutput, calls=%fused_computation.180 | convolution fusion | flops 6442450944 | bytes 8388608 | tf_op jit(solution)/shard_map/dot_general | solution.py:38
  360.9 19.1 %collective-permute-done = f32[256,1024]{0,1:T(8,128)S(1)} collective-permute-done((f32[256,1024]{0,1:T(8,128)S(1)}, f32[256,1024]{0,1:T(8,128)S(1)}, u32[]{:S(2)}, u32[]{:S(2)}) %collective-permute-start) | collective-permute-done | bytes 1048608 | tf_op jit(solution)/shard_map/ppermute | solution.py:65
  382.0 2.4 constant_dynamic-update-slice_fusion.27
  384.4 44.2 %collective-permute-done.2 = f32[256,1024]{0,1:T(8,128)} collective-permute-done((f32[256,1024]{0,1:T(8,128)S(1)}, f32[256,1024]{0,1:T(8,128)}, u32[]{:S(2)}, u32[]{:S(2)}) %collective-permute-start.2) | collective-permute-done | bytes 1048608 | tf_op jit(solution)/shard_map/ppermute | solution.py:65
  428.6 2.3 constant_dynamic-update-slice_fusion.26
  430.9 5.6 copy.44
  436.5 4.4 fusion
  442.9 11.7 %cholesky.222 = f32[128,128]{1,0:T(8,128)S(1)} custom-call(f32[128,128]{1,0:T(8,128)S(1)} %cholesky.577), custom_call_target="Cholesky" | custom-call | tf_op jit(solution)/shard_map/jit(cholesky)/cholesky | solution.py:74
  454.8 9.8 %custom-call.62 = f32[1,128,128]{1,2,0:T(8,128)S(1)} custom-call(f32[1,128,128]{2,1,0:T(8,128)S(1)} %get-tuple-element.47), custom_call_target="InvertDiagBlocksLowerTriangular" | custom-call | tf_op jit(solution)/shard_map/jit(cholesky)/cholesky | solution.py:74
  467.9 11.7 %cholesky.243 = f32[128,128]{1,0:T(8,128)S(1)} custom-call(f32[128,128]{1,0:T(8,128)S(1)} %cholesky.581), custom_call_target="Cholesky" | custom-call | tf_op jit(solution)/shard_map/jit(cholesky)/cholesky | solution.py:74
  479.7 2.9 cholesky.254
  482.6 9.8 %custom-call.63 = f32[1,128,128]{1,2,0:T(8,128)S(1)} custom-call(f32[1,128,128]{2,1,0:T(8,128)S(1)} %get-tuple-element.45), custom_call_target="InvertDiagBlocksLowerTriangular" | custom-call | tf_op jit(solution)/shard_map/jit(cholesky)/cholesky | solution.py:74
  495.3 2.7 slice_subtract_fusion.1
  498.0 11.7 %cholesky.466 = f32[128,128]{1,0:T(8,128)S(1)} custom-call(f32[128,128]{1,0:T(8,128)S(1)} %cholesky.586), custom_call_target="Cholesky" | custom-call | tf_op jit(solution)/shard_map/jit(cholesky)/cholesky | solution.py:74
  509.8 9.8 %custom-call.64 = f32[1,128,128]{1,2,0:T(8,128)S(1)} custom-call(f32[1,128,128]{2,1,0:T(8,128)S(1)} %get-tuple-element.43), custom_call_target="InvertDiagBlocksLowerTriangular" | custom-call | tf_op jit(solution)/shard_map/jit(cholesky)/cholesky | solution.py:74
  521.5 3.3 slice_subtract_fusion.2
  524.8 11.7 %cholesky.485 = f32[128,128]{1,0:T(8,128)S(1)} custom-call(f32[128,128]{1,0:T(8,128)S(1)} %cholesky.591), custom_call_target="Cholesky" | custom-call | tf_op jit(solution)/shard_map/jit(cholesky)/cholesky | solution.py:74
  536.7 9.8 %custom-call.65 = f32[1,128,128]{1,2,0:T(8,128)S(1)} custom-call(f32[1,128,128]{2,1,0:T(8,128)S(1)} %get-tuple-element.41), custom_call_target="InvertDiagBlocksLowerTriangular" | custom-call | tf_op jit(solution)/shard_map/jit(cholesky)/cholesky | solution.py:74
  548.3 3.1 slice_subtract_fusion.3
  551.4 11.9 %cholesky.504 = f32[128,128]{1,0:T(8,128)S(1)} custom-call(f32[128,128]{1,0:T(8,128)S(1)} %cholesky.596), custom_call_target="Cholesky" | custom-call | tf_op jit(solution)/shard_map/jit(cholesky)/cholesky | solution.py:74
  563.4 9.8 %custom-call.66 = f32[1,128,128]{1,2,0:T(8,128)S(1)} custom-call(f32[1,128,128]{2,1,0:T(8,128)S(1)} %get-tuple-element.39), custom_call_target="InvertDiagBlocksLowerTriangular" | custom-call | tf_op jit(solution)/shard_map/jit(cholesky)/cholesky | solution.py:74
  575.0 3.2 slice_subtract_fusion.4
  578.3 11.7 %cholesky.524 = f32[128,128]{1,0:T(8,128)S(1)} custom-call(f32[128,128]{1,0:T(8,128)S(1)} %cholesky.601), custom_call_target="Cholesky" | custom-call | tf_op jit(solution)/shard_map/jit(cholesky)/cholesky | solution.py:74
  590.1 9.8 %custom-call.67 = f32[1,128,128]{1,2,0:T(8,128)S(1)} custom-call(f32[1,128,128]{2,1,0:T(8,128)S(1)} %get-tuple-element.37), custom_call_target="InvertDiagBlocksLowerTriangular" | custom-call | tf_op jit(solution)/shard_map/jit(cholesky)/cholesky | solution.py:74
  601.6 3.1 slice_subtract_fusion.5
  604.7 11.7 %cholesky.544 = f32[128,128]{1,0:T(8,128)S(1)} custom-call(f32[128,128]{1,0:T(8,128)S(1)} %cholesky.606), custom_call_target="Cholesky" | custom-call | tf_op jit(solution)/shard_map/jit(cholesky)/cholesky | solution.py:74
  616.6 9.8 %custom-call.68 = f32[1,128,128]{1,2,0:T(8,128)S(1)} custom-call(f32[1,128,128]{2,1,0:T(8,128)S(1)} %get-tuple-element.35), custom_call_target="InvertDiagBlocksLowerTriangular" | custom-call | tf_op jit(solution)/shard_map/jit(cholesky)/cholesky | solution.py:74
  628.0 2.2 slice_subtract_fusion.6
  630.2 11.7 %cholesky.562 = f32[128,128]{1,0:T(8,128)S(1)} custom-call(f32[128,128]{1,0:T(8,128)S(1)} %slice_subtract_fusion.6), custom_call_target="Cholesky" | custom-call | tf_op jit(solution)/shard_map/jit(cholesky)/cholesky | solution.py:74
  652.3 4.9 select_select_fusion
  657.3 2.3 sub.15
  659.6 28.3 %while.1 = (s32[]{:T(128)}, f32[1024,1024]{0,1:T(8,128)}, s32[8,2]{0,1:T(2,128)S(1)}, f32[8,128,128]{2,1,0:T(8,128)}, s32[]{:T(128)}) while((s32[]{:T(128)}, f32[1024,1024]{0,1:T(8,128)}, s32[8,2]{0,1:T(2,128)S(1)}, f32[8,128,128]{2,1,0:T(8,128)}, s32[]{:T(128)}) %tuple.39), condition=%wide.while_cond, body=%wide.while_body.sunk | while | flops 2 | bytes 393829 | solution.py:79
  663.9 2.2 dynamic-slice.7
  667.5 2.2 dynamic-slice.7
  671.0 2.2 dynamic-slice.7
  681.6 2.2 dynamic-slice.7
  688.0 79.4 %custom-call.69 = f32[8,128,128]{1,2,0:T(8,128)S(1)} custom-call(f32[8,128,128]{2,1,0:T(8,128)} %get-tuple-element.9), custom_call_target="InvertDiagBlocksLowerTriangular" | custom-call | tf_op jit(solution)/shard_map/triangular_solve | solution.py:79
  779.6 6.8 fusion.87
  (162 shorter events, 68.4 us)
Async XLA Ops:
  7.2 56.0 %all-gather.3.cloned.1.call-start = ((), (), s32[]{:S(2)}) async-start(), calls=%async_computation.2 | async-start | bytes 5242880 | tf_op jit(solution)/shard_map/all_gather | solution.py:48
  7.9 261.7 %all-reduce.3.cloned.1.call-start = ((), (), s32[]{:S(2)}) async-start(), calls=%async_computation.3 | async-start | bytes 6291456 | tf_op jit(solution)/shard_map/psum | solution.py:9
  274.3 3.1 copy-start.4
  287.3 55.0 %all-to-all-start = ((f32[4,256,1024]{2,1,0:T(8,128)}), f32[4,256,1024]{2,1,0:T(8,128)}, u32[]{:S(2)}, u32[]{:S(2)}) async-start(f32[4,256,1024]{2,1,0:T(8,128)} %fusion.85), calls=%async_computation | async-start | bytes 8388608 | tf_op jit(solution)/shard_map/all_to_all | solution.py:23
  292.2 365.1 %reduce-scatter.2.cloned.1.call-start = ((), (), s32[]{:S(2)}) async-start(), calls=%async_computation.4 | async-start | bytes 5242880 | tf_op jit(solution)/shard_map/reduce_scatter | solution.py:51
  345.3 7.1 copy-start
  345.4 7.1 copy-start.3
  349.2 30.8 %collective-permute-start = (f32[256,1024]{0,1:T(8,128)S(1)}, f32[256,1024]{0,1:T(8,128)S(1)}, u32[]{:S(2)}, u32[]{:S(2)}) collective-permute-start(f32[256,1024]{0,1:T(8,128)S(1)} %get-tuple-element.31), channel_id=1, source_target_pairs={{0,1},{1,2},{2,3},{3,0},{4,5},{5,6},{6,7},{7,4},{8,9},{9,10},{10,1... | collective-permute-start | bytes 3145736 | tf_op jit(solution)/shard_map/ppermute | solution.py:65
  349.8 32.2 %collective-permute-start.1 = (f32[256,1024]{0,1:T(8,128)S(1)}, f32[256,1024]{0,1:T(8,128)}, u32[]{:S(2)}, u32[]{:S(2)}) collective-permute-start(f32[256,1024]{0,1:T(8,128)S(1)} %get-tuple-element.31), channel_id=1, source_target_pairs={{0,3},{1,0},{2,1},{3,2},{4,7},{5,4},{6,5},{7,6},{8,11},{9,8},{10,9... | collective-permute-start | bytes 3145736 | tf_op jit(solution)/shard_map/ppermute | solution.py:70
  360.8 418.7 %all-gather.5.cloned.1.call-start = ((), (), s32[]{:S(2)}) async-start(), calls=%async_computation.5 | async-start | bytes 5242880 | tf_op jit(solution)/shard_map/all_gather | solution.py:82
  380.0 48.6 %collective-permute-start.2 = (f32[256,1024]{0,1:T(8,128)S(1)}, f32[256,1024]{0,1:T(8,128)}, u32[]{:S(2)}, u32[]{:S(2)}) collective-permute-start(f32[256,1024]{0,1:T(8,128)S(1)} %collective-permute-done), channel_id=1, source_target_pairs={{0,1},{1,2},{2,3},{3,0},{4,5},{5,6},{6,7},{7,4},{8,9},{9,10},{10,1... | collective-permute-start | bytes 3145736 | tf_op jit(solution)/shard_map/ppermute | solution.py:65
  440.9 2.0 copy-start.1
  652.3 5.0 copy-start.2
Sparse Core Ops, SparseCore 0:
  9.8 53.3 all-gather.2
  78.6 190.9 all-reduce.2
  360.9 72.0 reduce-scatter.1
  659.7 47.5 all-gather.4
